TPU v7x, 32 devices: a whole 2x2x4 slice. The times are simulated.
32 devices in a mesh: kpt: 2 (over x), row: 8 (over z, y), col: 2 (over core).
Axes of the slice: x: 2, y: 2, z: 4, core: 2. Of those that a mesh axis runs over, the one named last changes fastest.
Arguments:
- wannier: float32 [64, 32, 1024], P('kpt', ('row', 'col')), parts along dimension 0, may hold values from -6 to 6
- pairs: int32 [384, 2], replicated, may hold values from 0 to 31, as said below
- gmap: int32 [8192], replicated, may hold values from 1 to 32767, as said below
- screened: bfloat16 [4, 2, 8192, 8192], P('kpt', None, 'row', 'col'), parts along dimension 0, may hold values from -0.046875 to 0.046875
Outputs:
- coulomb: float32 [2, 2, 768, 384], P(None, None, ('kpt', 'row', 'col')), parts along dimension 2
There are 2 independent parts, one for each index of `kpt`. A program takes and returns all parts, laid end to end along the dimension named above; an argument that names none is the same for every part. Nothing has to cross between parts.
Inputs may be any that keep to these rules, and one draw needn't show every extreme that they name: `gmap`: 8192 distinct flat cells of the grid; cell 0 is never among them. `pairs`: in each row the first Wannier function is no greater than the second; no two rows are equal.
All inputs are finite; a program needn't handle non-finite values.
Results may differ from a plain program's by a relative error of at most 0.0082.
Values may be sent and summed in bfloat16 or wider, within the bound.
No kernel may reach another device: no remote copies, remote signals or barrier semaphores. Data moves between devices by JAX's collectives and lax.ppermute only.
A program may use at most 128 MiB of HBM per device.

v0:
```python
import math
import jax
import jax.numpy as jnp
from jax import lax
from jax.sharding import PartitionSpec as P

NW = 32
GX = 32
NG = 8192
NP = 384


def line_tables(side_len):
    positions = jnp.arange(side_len, dtype=jnp.int32)
    phase_index = positions[:, None] * positions[None, :] % side_len
    angles = phase_index.astype(jnp.float32) * (2.0 * math.pi / side_len)
    return (jnp.cos(angles), jnp.sin(angles))


def plane_transform(density):
    cosine, sine_table = line_tables(GX)
    highest = lax.Precision.HIGHEST
    shaped = density.reshape(-1, GX, GX)
    real_z = jnp.einsum("nyz,kz->nyk", shaped, cosine, precision=highest)
    imag_z = -jnp.einsum("nyz,kz->nyk", shaped, sine_table, precision=highest)
    new_real = jnp.einsum("jy,nyk->njk", cosine, real_z, precision=highest) + jnp.einsum(
        "jy,nyk->njk", sine_table, imag_z, precision=highest
    )
    new_imag = jnp.einsum("jy,nyk->njk", cosine, imag_z, precision=highest) - jnp.einsum(
        "jy,nyk->njk", sine_table, real_z, precision=highest
    )
    return (new_real.reshape(density.shape), new_imag.reshape(density.shape))


def line_transform(real_part, imag_part):
    cosine, sine_table = line_tables(GX)
    highest = lax.Precision.HIGHEST
    new_real = jnp.einsum("kn,pny->pky", cosine, real_part, precision=highest) + jnp.einsum(
        "kn,pny->pky", sine_table, imag_part, precision=highest
    )
    new_imag = jnp.einsum("kn,pny->pky", cosine, imag_part, precision=highest) - jnp.einsum(
        "kn,pny->pky", sine_table, real_part, precision=highest
    )
    return (new_real, new_imag)


def right_columns(screened, segment):
    w_real = screened[:, 0]
    w_imag = screened[:, 1]
    real_real = jnp.einsum("fgh,bh->fgb", w_real, segment[0], preferred_element_type=jnp.float32)
    imag_imag = jnp.einsum("fgh,bh->fgb", w_imag, segment[1], preferred_element_type=jnp.float32)
    real_imag = jnp.einsum("fgh,bh->fgb", w_real, segment[1], preferred_element_type=jnp.float32)
    imag_real = jnp.einsum("fgh,bh->fgb", w_imag, segment[0], preferred_element_type=jnp.float32)
    return jnp.stack([real_real - imag_imag, real_imag + imag_real], axis=1)


def shards(wannier, pairs, gmap, screened):
    planes = wannier.shape[1]
    grid_cells = wannier.shape[2]
    members = jnp.arange(NW, dtype=jnp.int32)[None, :]
    pick_first = (pairs[:, 0:1] == members).astype(jnp.float32)
    pick_second = (pairs[:, 1:2] == members).astype(jnp.float32)
    flat_rows = wannier.reshape(NW, -1)
    highest = lax.Precision.HIGHEST
    density = jnp.dot(pick_first, flat_rows, precision=highest) * jnp.dot(
        pick_second, flat_rows, precision=highest
    )
    density = density.reshape(NP, planes, grid_cells)
    arrived = lax.all_to_all(density, ("row", "col"), split_axis=0, concat_axis=1, tiled=True)
    real_part, imag_part = plane_transform(arrived)
    real_part, imag_part = line_transform(real_part, imag_part)
    owned = real_part.shape[0]
    norm_factor = 1.0 / math.sqrt(GX * GX * GX)
    rho_real = jnp.take(real_part.reshape(owned, -1), gmap, axis=1) * norm_factor
    rho_imag = jnp.take(imag_part.reshape(owned, -1), gmap, axis=1) * norm_factor
    rho = jnp.stack([rho_real, rho_imag], axis=0).astype(jnp.bfloat16)
    row_span = screened.shape[2]
    halves = lax.all_to_all(rho, "col", split_axis=2, concat_axis=1, tiled=True)
    screened_rho = right_columns(screened, lax.all_gather(halves, "row", axis=1, tiled=True))
    blocks = lax.all_to_all(rho, "row", split_axis=2, concat_axis=1, tiled=True)
    blocks = blocks.reshape(2, lax.axis_size("row"), owned, row_span)
    left_panel = lax.all_gather(blocks, "col", axis=2, tiled=True).reshape(2, NP, row_span)
    left_wide = left_panel.astype(jnp.float32)
    u_real = jnp.einsum(
        "ag,fgb->fab", left_wide[0], screened_rho[:, 0], precision=highest
    ) + jnp.einsum("ag,fgb->fab", left_wide[1], screened_rho[:, 1], precision=highest)
    u_imag = jnp.einsum(
        "ag,fgb->fab", left_wide[0], screened_rho[:, 1], precision=highest
    ) - jnp.einsum("ag,fgb->fab", left_wide[1], screened_rho[:, 0], precision=highest)
    partial_terms = jnp.stack([u_real, u_imag], axis=1) / math.sqrt(NG)
    summed = lax.psum(partial_terms, ("row", "col"))
    share_rows = NP // lax.axis_size(("row", "col"))
    return lax.dynamic_slice_in_dim(
        summed, lax.axis_index(("row", "col")) * share_rows, share_rows, 2
    )


def solution(mesh):
    return jax.shard_map(
        shards,
        mesh=mesh,
        in_specs=(P("kpt", ("row", "col"), None), P(), P(), P("kpt", None, "row", "col")),
        out_specs=P(None, None, ("kpt", "row", "col"), None),
        check_vma=False,
    )
```

profile of v0, /device:TPU:0, one launch (start us, length us, event | category | flops | bytes accessed | tf_op | source)
XLA Modules:
  0.0 687.3 jit_solution(8600309741713015094)
XLA Ops:
  6.5 0.8 slice_reduce_fusion
  7.3 1.0 copy.93
  8.3 1.4 fusion.54
  9.8 1.5 convolution_multiply_fusion
  11.3 3.8 reshape.35
  15.1 7.5 %all-to-all-start = ((f32[384,2,1024]{2,1,0:T(2,128)}), f32[384,2,1024]{2,1,0:T(2,128)S(1)}, u32[]{:S(2)}, u32[]{:S(2)}) async-start(f32[384,2,1024]{2,1,0:T(2,128)} %reshape.35), calls=%async_computation | async-start | bytes 6291456 | tf_op jit(solution)/shard_map/all_to_all | solution.py:69
  22.6 0.0 all-gather.5.cloned.1.call-start
  22.7 0.0 copy-done.4
  22.7 59.1 %all-to-all-done = f32[384,2,1024]{2,1,0:T(2,128)S(1)} async-done(((f32[384,2,1024]{2,1,0:T(2,128)}), f32[384,2,1024]{2,1,0:T(2,128)S(1)}, u32[]{:S(2)}, u32[]{:S(2)}) %all-to-all-start) | async-done | bytes 3145760 | tf_op jit(solution)/shard_map/all_to_all | solution.py:69
  81.9 1.0 copy.70
  82.9 2.4 copy.71
  85.3 7.6 %reshape.36 = f32[768,32,32]{2,1,0:T(8,128)} reshape(f32[24,16,2,1024]{3,2,1,0:T(2,128)S(1)} %copy.71) | data formatting | bytes 6291456 | tf_op jit(solution)/shard_map/reshape | solution.py:23
  92.9 9.2 %copy.72 = f32[768,32,32]{0,2,1:T(8,128)S(1)} copy(f32[768,32,32]{2,1,0:T(8,128)} %reshape.36) | data formatting | bytes 6291456 | tf_op jit(solution)/shard_map/reshape | solution.py:23
  102.1 3.0 convolution_negate_fusion
  105.1 3.0 fusion.72
  108.1 4.9 fusion.22
  113.1 5.2 fusion.24
  118.2 6.7 add_bitcast_fusion.1
  125.0 5.5 subtract_bitcast_fusion.1
  130.5 10.6 %copy.79 = f32[768,32,32]{2,1,0:T(8,128)} copy(f32[768,32,32]{0,1,2:T(8,128)S(1)} %subtract_bitcast_fusion.1) | data formatting | bytes 6291456 | tf_op jit(solution)/shard_map/sub | solution.py:29
  141.1 9.4 %reshape.38 = f32[24,32,1024]{2,1,0:T(8,128)S(1)} reshape(f32[768,32,32]{2,1,0:T(8,128)} %copy.79) | data formatting | bytes 6291456 | tf_op jit(solution)/shard_map/reshape | solution.py:32
  150.4 5.5 fusion.66
  155.9 11.4 %copy.76 = f32[768,32,32]{2,1,0:T(8,128)} copy(f32[768,32,32]{0,1,2:T(8,128)} %add_bitcast_fusion.1) | data formatting | bytes 6291456 | tf_op jit(solution)/shard_map/add | solution.py:26
  167.3 10.7 %reshape.37 = f32[24,32,1024]{2,1,0:T(8,128)} reshape(f32[768,32,32]{2,1,0:T(8,128)} %copy.76) | data formatting | bytes 6291456 | tf_op jit(solution)/shard_map/reshape | solution.py:32
  178.0 5.9 fusion.69
  184.0 5.5 subtract_bitcast_fusion
  189.5 5.6 add_bitcast_fusion
  195.1 10.3 %copy.89 = f32[24,32,1024]{0,2,1:T(8,128)} copy(f32[24,32,1024]{2,1,0:T(8,128)} %add_bitcast_fusion) | data formatting | bytes 6291456 | tf_op jit(solution)/shard_map/reshape | solution.py:74
  205.4 0.0 copy-done.2
  205.4 8.6 %copy.90 = f32[24,32,1024]{0,2,1:T(8,128)} copy(f32[24,32,1024]{2,1,0:T(8,128)S(1)} %copy-done.2) | data formatting | bytes 6291456 | tf_op jit(solution)/shard_map/reshape | solution.py:75
  214.0 33.6 %gather_fusion = f32[8192,24]{1,0:T(8,128)} fusion(f32[24,32768]{0,1:T(8,128)} %bitcast.144, s32[8192]{0:T(1024)S(1)} %fusion.57), kind=kCustom, calls=%fused_computation.clone | custom fusion | bytes 1605632 | tf_op jit(solution)/shard_map/jit(_take)/gather | solution.py:74
  247.6 33.6 %gather_fusion.1 = f32[8192,24]{1,0:T(8,128)} fusion(f32[24,32768]{0,1:T(8,128)} %bitcast.143, s32[8192]{0:T(1024)S(1)} %fusion.57), kind=kCustom, calls=%fused_computation.1.clone | custom fusion | bytes 1605632 | tf_op jit(solution)/shard_map/jit(_take)/gather | solution.py:75
  281.3 7.2 %fusion.30 = (bf16[1,24,8192]{1,2,0:T(8,128)(2,1)S(1)}, bf16[1,24,8192]{1,2,0:T(8,128)(2,1)S(1)}) fusion(f32[8192,24]{1,0:T(8,128)} %gather_fusion, pred[8192]{0:T(1024)(128)(4,1)S(1)} %compare_and_fusion, f32[8192,24]{1,0:T(8,128)} %gather_fusion.1), kind=kLoop, calls=%fused_computation.43 | loop fusion | flops 1179648 | bytes 2367488 | tf_op jit(solution)/shard_map/stack | solution.py:76
  288.4 0.9 pad_maximum_fusion
  289.4 35.5 %copy.108 = bf16[2,24,8192]{1,0,2:T(2,128)(2,1)} copy(bf16[2,24,8192]{1,2,0:T(8,128)(2,1)S(1)} %pad_maximum_fusion) | data formatting | bytes 1572864 | tf_op jit(solution)/shard_map/stack | solution.py:76
  324.9 6.6 reshape.71
  331.5 35.8 %all_to_all.48 = bf16[8,2,24576]{2,1,0:T(2,128)(2,1)S(1)} all-to-all(bf16[8,2,24576]{2,1,0:T(2,128)(2,1)S(1)} %reshape.71), channel_id=1, replica_groups=mesh['kpt'=2,'row'=8,'col'=2] {'row'}, dimensions={0} | all-to-all | bytes 1572864 | tf_op jit(solution)/shard_map/all_to_all | solution.py:80
  367.3 6.9 %reshape.72 = bf16[8192,2,24]{2,1,0:T(2,128)(2,1)} reshape(bf16[8,2,24576]{2,1,0:T(2,128)(2,1)S(1)} %all_to_all.48) | data formatting | bytes 1572864
  374.3 10.3 %copy.87 = bf16[2,24,8,1024]{3,1,2,0:T(8,128)(2,1)} copy(bf16[2,24,8,1024]{1,0,3,2:T(2,128)(2,1)} %bitcast.145) | data formatting | bytes 1572864 | tf_op jit(solution)/shard_map/all_to_all | solution.py:80
  384.6 0.0 all-gather.5.cloned.1.call-update
  384.6 0.0 all-gather.3.cloned.1.call-start
  384.6 10.2 %copy.109 = bf16[2,24,8192]{1,0,2:T(2,128)(2,1)} copy(bf16[2,24,8192]{1,2,0:T(8,128)(2,1)} %copy-done) | data formatting | bytes 1572864 | tf_op jit(solution)/shard_map/stack | solution.py:76
  394.8 7.0 %reshape.73 = bf16[2,2,98304]{2,1,0:T(2,128)(2,1)S(1)} reshape(bf16[8192,2,24]{2,1,0:T(2,128)(2,1)} %bitcast.147) | data formatting | bytes 1572864
  401.9 4.4 all_to_all.49
  406.2 7.3 %reshape.74 = bf16[8192,2,24]{2,1,0:T(2,128)(2,1)} reshape(bf16[2,2,98304]{2,1,0:T(2,128)(2,1)S(1)} %all_to_all.49) | data formatting | bytes 1572864
  413.6 9.5 %copy.83 = bf16[2,24,2,4096]{3,1,2,0:T(8,128)(2,1)} copy(bf16[2,24,2,4096]{1,0,3,2:T(2,128)(2,1)} %bitcast.146) | data formatting | bytes 1572864 | tf_op jit(solution)/shard_map/all_to_all | solution.py:78
  423.0 0.0 all-gather.3.cloned.1.call-update
  423.1 0.0 all-reduce.2.cloned.1.call-start
  423.1 0.0 all-gather.5.cloned.1.call-done
  423.1 1.5 fusion.129
  424.7 96.3 %all-gather.3.cloned.1.call-done = bf16[2,384,4096]{2,1,0:T(8,128)(2,1)} async-done(((bf16[2,48,4096]{2,1,0:T(8,128)(2,1)}), bf16[2,384,4096]{2,1,0:T(8,128)(2,1)}) %all-gather.3.cloned.1.call-update) | async-done | bytes 6291472 | tf_op jit(solution)/shard_map/all_gather | solution.py:79
  521.0 11.4 %fusion = f32[384,2,1024]{2,0,1:T(8,128)S(1)} fusion(bf16[2,2,1024,4096]{3,2,1,0:T(8,128)(2,1)} %param.9, bf16[2,384,4096]{2,1,0:T(8,128)(2,1)} %all-gather.3.cloned.1.call-done), kind=kOutput, calls=%fused_computation.2 | convolution fusion | flops 6442450944 | bytes 23068672 | tf_op jit(solution)/shard_map/fgh,bh->fgb/dot_general | solution.py:53
  532.4 11.2 %fusion.39 = f32[384,2,1024]{2,0,1:T(8,128)S(1)} fusion(f32[384,2,1024]{2,0,1:T(8,128)S(1)} %fusion, bf16[2,2,1024,4096]{3,2,1,0:T(8,128)(2,1)} %param.9, bf16[2,384,4096]{2,1,0:T(8,128)(2,1)} %all-gather.3.cloned.1.call-done), kind=kOutput, calls=%fused_computation.47 | convolution fusion | flops 6443237376 | bytes 26214400 | tf_op jit(solution)/shard_map/fgh,bh->fgb/dot_general | solution.py:52
  543.6 2.6 fusion.14
  546.2 2.6 fusion.16
  548.9 12.6 %fusion.2 = f32[384,2,1024]{2,0,1:T(8,128)} fusion(bf16[2,2,1024,4096]{3,2,1,0:T(8,128)(2,1)} %param.9, bf16[2,384,4096]{2,1,0:T(8,128)(2,1)} %all-gather.3.cloned.1.call-done), kind=kOutput, calls=%fused_computation.4 | convolution fusion | flops 6442450944 | bytes 23068672 | tf_op jit(solution)/shard_map/fgh,bh->fgb/dot_general | solution.py:51
  561.5 12.1 %fusion.36 = f32[384,2,1024]{2,0,1:T(8,128)S(1)} fusion(f32[384,2,1024]{2,0,1:T(8,128)} %fusion.2, bf16[2,2,1024,4096]{3,2,1,0:T(8,128)(2,1)} %param.9, bf16[2,384,4096]{2,1,0:T(8,128)(2,1)} %all-gather.3.cloned.1.call-done), kind=kOutput, calls=%fused_computation.46 | convolution fusion | flops 6443237376 | bytes 26214400 | tf_op jit(solution)/shard_map/fgh,bh->fgb/dot_general | solution.py:50
  573.6 2.7 fusion.48
  576.3 2.7 fusion.51
  579.0 1.6 maximum_multiply_fusion
  580.6 0.0 all-reduce.2.cloned.1.call-update
  580.6 97.4 %all-reduce.2.cloned.1.call-done = f32[2,2,384,384]{2,3,0,1:T(8,128)} async-done(((f32[2,2,384,384]{2,3,0,1:T(8,128)}), f32[2,2,384,384]{2,3,0,1:T(8,128)}) %all-reduce.2.cloned.1.call-update) | async-done | bytes 2359312 | tf_op jit(solution)/shard_map/psum | solution.py:91
  678.0 1.7 constant_dynamic-slice_fusion
  679.6 0.9 copy.88
  (10 shorter events, 0.0 us)
Async XLA Ops:
  15.1 7.6 %copy-start.4 = (s32[8192]{0:T(1024)S(1)}, s32[8192]{0:T(1024)}, u32[]{:S(2)}) copy-start(s32[8192]{0:T(1024)} %param.8) | copy-start | bytes 98308
  15.1 66.8 %all-to-all-start = ((f32[384,2,1024]{2,1,0:T(2,128)}), f32[384,2,1024]{2,1,0:T(2,128)S(1)}, u32[]{:S(2)}, u32[]{:S(2)}) async-start(f32[384,2,1024]{2,1,0:T(2,128)} %reshape.35), calls=%async_computation | async-start | bytes 6291456 | tf_op jit(solution)/shard_map/all_to_all | solution.py:69
  22.6 400.5 %all-gather.5.cloned.1.call-start = ((), (), s32[]{:S(2)}) async-start(), calls=%async_computation.4 | async-start | bytes 2359296 | tf_op jit(solution)/shard_map/all_gather | solution.py:82
  178.0 6.0 copy-start.1
  178.0 6.0 copy-start.3
  195.1 10.3 %copy-start.2 = (f32[24,32,1024]{2,1,0:T(8,128)S(1)}, f32[24,32,1024]{2,1,0:T(8,128)}, u32[]{:S(2)}) copy-start(f32[24,32,1024]{2,1,0:T(8,128)} %subtract_bitcast_fusion) | copy-start | bytes 9437188
  289.4 35.5 %copy-start = (bf16[2,24,8192]{1,2,0:T(8,128)(2,1)}, bf16[2,24,8192]{1,2,0:T(8,128)(2,1)S(1)}, u32[]{:S(2)}) copy-start(bf16[2,24,8192]{1,2,0:T(8,128)(2,1)S(1)} %pad_maximum_fusion) | copy-start | bytes 2359300
  384.6 136.4 %all-gather.3.cloned.1.call-start = ((), (), s32[]{:S(2)}) async-start(), calls=%async_computation.3 | async-start | bytes 7077888 | tf_op jit(solution)/shard_map/all_gather | solution.py:79
  423.1 254.9 %all-reduce.2.cloned.1.call-start = ((), (), s32[]{:S(2)}) async-start(), calls=%async_computation.5 | async-start | bytes 4718592 | tf_op jit(solution)/shard_map/psum | solution.py:91
Sparse Core Ops, SparseCore 0:
  384.7 8.8 all-gather.4
  423.2 97.7 all-gather.2
  580.7 97.1 all-reduce.1
where the time goes:
time: 696 us; the launch traced here: 687 us
  waiting for transfers between devices  253 us (36%)
  local copies, waits for them, and re-layouts  251 us (36%)
  matrix products  112 us (16%)
  blocking collectives  40.2 us (6%)
  between operations  13.7 us (2%)
  other arithmetic  9.75 us (1%)
  starting transfers between devices  7.67 us (1%)
    psum x1, waiting for transfers between devices, shards(): summed = lax.psum(partial_terms, ('row', 'col'))  97.4 us
    all_gather x1, waiting for transfers between devices, shards(): lax.all_gather(halves, 'row', axis=1, tiled=True)  96.3 us
    all_to_all x1, waiting for transfers between devices, shards(): lax.all_to_all(density, ('row', 'col'), split_axis=0, concat_axis=1, tile...  59.1 us
    another operation x2, local copies, waits for them, and re-layouts, shards(): rho = jnp.stack([rho_real, rho_imag], axis=0).astype(jnp.bfloat16)  45.7 us
    all_to_all x1, blocking collectives, shards(): blocks = lax.all_to_all(rho, 'row', split_axis=2, concat_axis=1, tiled=True)  35.8 us
    gather x1, local copies, waits for them, and re-layouts, shards(): jnp.take(imag_part.reshape(owned, -1), gmap, axis=1) * norm_factor  33.6 us
    gather x1, local copies, waits for them, and re-layouts, shards(): jnp.take(real_part.reshape(owned, -1), gmap, axis=1) * norm_factor  33.6 us
    unnamed x15, local copies, waits for them, and re-layouts  29 us
  transfers between devices with their start and end apart: 4, of which 3 were waited for; matrix products, arithmetic and copies ran while one was open for 5% of the time, Pallas kernels for 0%

commit v1 on v0

--- a/solution.py
+++ b/solution.py
@@ -88,7 +88,7 @@
         "ag,fgb->fab", left_wide[0], screened_rho[:, 1], precision=highest
     ) - jnp.einsum("ag,fgb->fab", left_wide[1], screened_rho[:, 0], precision=highest)
     partial_terms = jnp.stack([u_real, u_imag], axis=1) / math.sqrt(NG)
-    summed = lax.psum(partial_terms, ("row", "col"))
+    summed = lax.psum(lax.psum(partial_terms, "col"), "row")
     share_rows = NP // lax.axis_size(("row", "col"))
     return lax.dynamic_slice_in_dim(
         summed, lax.axis_index(("row", "col")) * share_rows, share_rows, 2

time: 696 us -> 732 us (1.052)
  waiting for transfers between devices: 253 us -> 289 us
    psum x1 -> x2, waiting for transfers between devices: 97.4 us -> 133 us  [shards(): summed = lax.psum(lax.psum(partial_terms, 'col'), 'row')]
  transfers between devices with their start and end apart: 4 -> 5, of which waited for: 3 -> 4; matrix products, arithmetic and copies ran while one was open for 5% -> 5% of each run, Pallas kernels for 0% -> 0%
where the time goes in v1:
time: 732 us; the launch traced here: 723 us
  waiting for transfers between devices  289 us (39%)
  local copies, waits for them, and re-layouts  251 us (34%)
  matrix products  112 us (15%)
  blocking collectives  40.2 us (5%)
  between operations  13.6 us (2%)
  other arithmetic  9.75 us (1%)
  starting transfers between devices  7.71 us (1%)
    psum x2, waiting for transfers between devices, shards(): summed = lax.psum(lax.psum(partial_terms, 'col'), 'row')  133 us
    all_gather x1, waiting for transfers between devices, shards(): lax.all_gather(halves, 'row', axis=1, tiled=True)  96.3 us
    all_to_all x1, waiting for transfers between devices, shards(): lax.all_to_all(density, ('row', 'col'), split_axis=0, concat_axis=1, tile...  59.1 us
    another operation x2, local copies, waits for them, and re-layouts, shards(): rho = jnp.stack([rho_real, rho_imag], axis=0).astype(jnp.bfloat16)  45.7 us
    all_to_all x1, blocking collectives, shards(): blocks = lax.all_to_all(rho, 'row', split_axis=2, concat_axis=1, tiled=True)  35.8 us
    gather x1, local copies, waits for them, and re-layouts, shards(): jnp.take(imag_part.reshape(owned, -1), gmap, axis=1) * norm_factor  33.6 us
    gather x1, local copies, waits for them, and re-layouts, shards(): jnp.take(real_part.reshape(owned, -1), gmap, axis=1) * norm_factor  33.6 us
    unnamed x15, local copies, waits for them, and re-layouts  29 us
  transfers between devices with their start and end apart: 5, of which 4 were waited for; matrix products, arithmetic and copies ran while one was open for 5% of the time, Pallas kernels for 0%

profile of v1, /device:TPU:0, one launch (start us, length us, event | category | flops | bytes accessed | tf_op | source)
XLA Modules:
  0.0 723.0 jit_solution(16120302236635844372)
XLA Ops:
  6.5 0.8 slice_reduce_fusion
  7.3 1.0 copy.93
  8.3 1.4 fusion.54
  9.8 1.5 convolution_multiply_fusion
  11.3 3.8 reshape.35
  15.1 7.5 %all-to-all-start = ((f32[384,2,1024]{2,1,0:T(2,128)}), f32[384,2,1024]{2,1,0:T(2,128)S(1)}, u32[]{:S(2)}, u32[]{:S(2)}) async-start(f32[384,2,1024]{2,1,0:T(2,128)} %reshape.35), calls=%async_computation | async-start | bytes 6291456 | tf_op jit(solution)/shard_map/all_to_all | solution.py:69
  22.6 0.0 all-gather.5.cloned.1.call-start
  22.7 59.1 %all-to-all-done = f32[384,2,1024]{2,1,0:T(2,128)S(1)} async-done(((f32[384,2,1024]{2,1,0:T(2,128)}), f32[384,2,1024]{2,1,0:T(2,128)S(1)}, u32[]{:S(2)}, u32[]{:S(2)}) %all-to-all-start) | async-done | bytes 3145760 | tf_op jit(solution)/shard_map/all_to_all | solution.py:69
  81.9 1.0 copy.70
  82.9 2.4 copy.71
  85.3 7.6 %reshape.36 = f32[768,32,32]{2,1,0:T(8,128)} reshape(f32[24,16,2,1024]{3,2,1,0:T(2,128)S(1)} %copy.71) | data formatting | bytes 6291456 | tf_op jit(solution)/shard_map/reshape | solution.py:23
  92.9 9.2 %copy.72 = f32[768,32,32]{0,2,1:T(8,128)S(1)} copy(f32[768,32,32]{2,1,0:T(8,128)} %reshape.36) | data formatting | bytes 6291456 | tf_op jit(solution)/shard_map/reshape | solution.py:23
  102.1 3.0 convolution_negate_fusion
  105.1 3.0 fusion.72
  108.1 4.9 fusion.22
  113.1 5.2 fusion.24
  118.2 6.7 add_bitcast_fusion.1
  125.0 5.5 subtract_bitcast_fusion.1
  130.5 10.6 %copy.79 = f32[768,32,32]{2,1,0:T(8,128)} copy(f32[768,32,32]{0,1,2:T(8,128)S(1)} %subtract_bitcast_fusion.1) | data formatting | bytes 6291456 | tf_op jit(solution)/shard_map/sub | solution.py:29
  141.1 9.4 %reshape.38 = f32[24,32,1024]{2,1,0:T(8,128)S(1)} reshape(f32[768,32,32]{2,1,0:T(8,128)} %copy.79) | data formatting | bytes 6291456 | tf_op jit(solution)/shard_map/reshape | solution.py:32
  150.4 5.5 fusion.66
  155.9 11.4 %copy.76 = f32[768,32,32]{2,1,0:T(8,128)} copy(f32[768,32,32]{0,1,2:T(8,128)} %add_bitcast_fusion.1) | data formatting | bytes 6291456 | tf_op jit(solution)/shard_map/add | solution.py:26
  167.3 10.7 %reshape.37 = f32[24,32,1024]{2,1,0:T(8,128)} reshape(f32[768,32,32]{2,1,0:T(8,128)} %copy.76) | data formatting | bytes 6291456 | tf_op jit(solution)/shard_map/reshape | solution.py:32
  178.0 5.9 fusion.69
  184.0 5.5 subtract_bitcast_fusion
  189.5 5.6 add_bitcast_fusion
  195.1 10.3 %copy.89 = f32[24,32,1024]{0,2,1:T(8,128)} copy(f32[24,32,1024]{2,1,0:T(8,128)} %add_bitcast_fusion) | data formatting | bytes 6291456 | tf_op jit(solution)/shard_map/reshape | solution.py:74
  205.4 8.6 %copy.90 = f32[24,32,1024]{0,2,1:T(8,128)} copy(f32[24,32,1024]{2,1,0:T(8,128)S(1)} %copy-done.2) | data formatting | bytes 6291456 | tf_op jit(solution)/shard_map/reshape | solution.py:75
  214.0 33.6 %gather_fusion = f32[8192,24]{1,0:T(8,128)} fusion(f32[24,32768]{0,1:T(8,128)} %bitcast.144, s32[8192]{0:T(1024)S(1)} %fusion.57), kind=kCustom, calls=%fused_computation.clone | custom fusion | bytes 1605632 | tf_op jit(solution)/shard_map/jit(_take)/gather | solution.py:74
  247.6 33.6 %gather_fusion.1 = f32[8192,24]{1,0:T(8,128)} fusion(f32[24,32768]{0,1:T(8,128)} %bitcast.143, s32[8192]{0:T(1024)S(1)} %fusion.57), kind=kCustom, calls=%fused_computation.1.clone | custom fusion | bytes 1605632 | tf_op jit(solution)/shard_map/jit(_take)/gather | solution.py:75
  281.3 7.2 fusion.30
  288.4 0.9 pad_maximum_fusion
  289.4 35.5 %copy.108 = bf16[2,24,8192]{1,0,2:T(2,128)(2,1)} copy(bf16[2,24,8192]{1,2,0:T(8,128)(2,1)S(1)} %pad_maximum_fusion) | data formatting | bytes 1572864 | tf_op jit(solution)/shard_map/stack | solution.py:76
  324.9 6.6 reshape.71
  331.5 35.8 %all_to_all.48 = bf16[8,2,24576]{2,1,0:T(2,128)(2,1)S(1)} all-to-all(bf16[8,2,24576]{2,1,0:T(2,128)(2,1)S(1)} %reshape.71), channel_id=1, replica_groups=mesh['kpt'=2,'row'=8,'col'=2] {'row'}, dimensions={0} | all-to-all | bytes 1572864 | tf_op jit(solution)/shard_map/all_to_all | solution.py:80
  367.3 6.9 reshape.72
  374.3 10.3 %copy.87 = bf16[2,24,8,1024]{3,1,2,0:T(8,128)(2,1)} copy(bf16[2,24,8,1024]{1,0,3,2:T(2,128)(2,1)} %bitcast.145) | data formatting | bytes 1572864 | tf_op jit(solution)/shard_map/all_to_all | solution.py:80
  384.6 0.0 all-gather.5.cloned.1.call-update
  384.6 0.0 all-gather.3.cloned.1.call-start
  384.6 10.2 %copy.109 = bf16[2,24,8192]{1,0,2:T(2,128)(2,1)} copy(bf16[2,24,8192]{1,2,0:T(8,128)(2,1)} %copy-done) | data formatting | bytes 1572864 | tf_op jit(solution)/shard_map/stack | solution.py:76
  394.8 7.0 reshape.73
  401.9 4.4 all_to_all.49
  406.2 7.3 %reshape.74 = bf16[8192,2,24]{2,1,0:T(2,128)(2,1)} reshape(bf16[2,2,98304]{2,1,0:T(2,128)(2,1)S(1)} %all_to_all.49) | data formatting | bytes 1572864
  413.6 9.5 %copy.83 = bf16[2,24,2,4096]{3,1,2,0:T(8,128)(2,1)} copy(bf16[2,24,2,4096]{1,0,3,2:T(2,128)(2,1)} %bitcast.146) | data formatting | bytes 1572864 | tf_op jit(solution)/shard_map/all_to_all | solution.py:78
  423.0 0.0 all-gather.3.cloned.1.call-update
  423.1 0.0 all-reduce.3.cloned.1.call-start
  423.1 0.0 all-gather.5.cloned.1.call-done
  423.1 1.5 fusion.129
  424.7 96.3 %all-gather.3.cloned.1.call-done = bf16[2,384,4096]{2,1,0:T(8,128)(2,1)} async-done(((bf16[2,48,4096]{2,1,0:T(8,128)(2,1)}), bf16[2,384,4096]{2,1,0:T(8,128)(2,1)}) %all-gather.3.cloned.1.call-update) | async-done | bytes 6291472 | tf_op jit(solution)/shard_map/all_gather | solution.py:79
  521.0 11.4 %fusion = f32[384,2,1024]{2,0,1:T(8,128)S(1)} fusion(bf16[2,2,1024,4096]{3,2,1,0:T(8,128)(2,1)} %param.9, bf16[2,384,4096]{2,1,0:T(8,128)(2,1)} %all-gather.3.cloned.1.call-done), kind=kOutput, calls=%fused_computation.2 | convolution fusion | flops 6442450944 | bytes 23068672 | tf_op jit(solution)/shard_map/fgh,bh->fgb/dot_general | solution.py:53
  532.3 11.2 %fusion.39 = f32[384,2,1024]{2,0,1:T(8,128)S(1)} fusion(f32[384,2,1024]{2,0,1:T(8,128)S(1)} %fusion, bf16[2,2,1024,4096]{3,2,1,0:T(8,128)(2,1)} %param.9, bf16[2,384,4096]{2,1,0:T(8,128)(2,1)} %all-gather.3.cloned.1.call-done), kind=kOutput, calls=%fused_computation.47 | convolution fusion | flops 6443237376 | bytes 26214400 | tf_op jit(solution)/shard_map/fgh,bh->fgb/dot_general | solution.py:52
  543.6 2.6 fusion.14
  546.2 2.6 fusion.16
  548.9 12.6 %fusion.2 = f32[384,2,1024]{2,0,1:T(8,128)} fusion(bf16[2,2,1024,4096]{3,2,1,0:T(8,128)(2,1)} %param.9, bf16[2,384,4096]{2,1,0:T(8,128)(2,1)} %all-gather.3.cloned.1.call-done), kind=kOutput, calls=%fused_computation.4 | convolution fusion | flops 6442450944 | bytes 23068672 | tf_op jit(solution)/shard_map/fgh,bh->fgb/dot_general | solution.py:51
  561.5 11.9 %fusion.36 = f32[384,2,1024]{2,0,1:T(8,128)S(1)} fusion(f32[384,2,1024]{2,0,1:T(8,128)} %fusion.2, bf16[2,2,1024,4096]{3,2,1,0:T(8,128)(2,1)} %param.9, bf16[2,384,4096]{2,1,0:T(8,128)(2,1)} %all-gather.3.cloned.1.call-done), kind=kOutput, calls=%fused_computation.46 | convolution fusion | flops 6443237376 | bytes 26214400 | tf_op jit(solution)/shard_map/fgh,bh->fgb/dot_general | solution.py:50
  573.3 2.7 fusion.48
  576.0 2.7 fusion.51
  578.7 1.6 maximum_multiply_fusion
  580.3 0.0 all-reduce.5.cloned.1.call-start
  580.4 20.0 %all-reduce.3.cloned.1.call-done = f32[2,2,384,384]{2,3,0,1:T(8,128)} async-done(((f32[2,2,384,384]{2,3,0,1:T(8,128)}), f32[2,2,384,384]{2,3,0,1:T(8,128)}) %all-reduce.3.cloned.1.call-update) | async-done | bytes 2359312 | tf_op jit(solution)/shard_map/psum | solution.py:91
  600.4 0.0 all-reduce.5.cloned.1.call-update
  600.4 113.2 %all-reduce.5.cloned.1.call-done = f32[2,2,384,384]{2,3,0,1:T(8,128)} async-done(((f32[2,2,384,384]{2,3,0,1:T(8,128)}), f32[2,2,384,384]{2,3,0,1:T(8,128)}) %all-reduce.5.cloned.1.call-update) | async-done | bytes 2359312 | tf_op jit(solution)/shard_map/psum | solution.py:91
  713.6 1.7 constant_dynamic-slice_fusion
  715.3 0.9 copy.88
  (13 shorter events, 0.1 us)
Async XLA Ops:
  15.1 7.6 %copy-start.4 = (s32[8192]{0:T(1024)S(1)}, s32[8192]{0:T(1024)}, u32[]{:S(2)}) copy-start(s32[8192]{0:T(1024)} %param.8) | copy-start | bytes 98308
  15.1 66.8 %all-to-all-start = ((f32[384,2,1024]{2,1,0:T(2,128)}), f32[384,2,1024]{2,1,0:T(2,128)S(1)}, u32[]{:S(2)}, u32[]{:S(2)}) async-start(f32[384,2,1024]{2,1,0:T(2,128)} %reshape.35), calls=%async_computation | async-start | bytes 6291456 | tf_op jit(solution)/shard_map/all_to_all | solution.py:69
  22.6 400.5 %all-gather.5.cloned.1.call-start = ((), (), s32[]{:S(2)}) async-start(), calls=%async_computation.4 | async-start | bytes 2359296 | tf_op jit(solution)/shard_map/all_gather | solution.py:82
  178.0 6.0 copy-start.1
  178.0 6.0 copy-start.3
  195.1 10.3 %copy-start.2 = (f32[24,32,1024]{2,1,0:T(8,128)S(1)}, f32[24,32,1024]{2,1,0:T(8,128)}, u32[]{:S(2)}) copy-start(f32[24,32,1024]{2,1,0:T(8,128)} %subtract_bitcast_fusion) | copy-start | bytes 9437188
  289.4 35.5 %copy-start = (bf16[2,24,8192]{1,2,0:T(8,128)(2,1)}, bf16[2,24,8192]{1,2,0:T(8,128)(2,1)S(1)}, u32[]{:S(2)}) copy-start(bf16[2,24,8192]{1,2,0:T(8,128)(2,1)S(1)} %pad_maximum_fusion) | copy-start | bytes 2359300
  384.6 136.4 %all-gather.3.cloned.1.call-start = ((), (), s32[]{:S(2)}) async-start(), calls=%async_computation.3 | async-start | bytes 7077888 | tf_op jit(solution)/shard_map/all_gather | solution.py:79
  423.1 177.3 %all-reduce.3.cloned.1.call-start = ((), (), s32[]{:S(2)}) async-start(), calls=%async_computation.5 | async-start | bytes 4718592 | tf_op jit(solution)/shard_map/psum | solution.py:91
  580.3 133.3 %all-reduce.5.cloned.1.call-start = ((), (), s32[]{:S(2)}) async-start(), calls=%async_computation.6 | async-start | bytes 4718592 | tf_op jit(solution)/shard_map/psum | solution.py:91
Sparse Core Ops, SparseCore 0:
  384.7 8.8 all-gather.4
  423.2 97.7 all-gather.2
  580.5 19.9 all-reduce.2
  603.8 109.7 all-reduce.4
